TPU v7x, 32 devices: a whole 2x2x4 slice. The times are simulated.
32 devices in a mesh: row: 8 (over z, core), col: 4 (over y, x).
Axes of the slice: x: 2, y: 2, z: 4, core: 2. Of those that a mesh axis runs over, the one named last changes fastest.
Arguments:
- tensor: bfloat16 [512, 2048, 256], P(('row', 'col')), may hold values from -6 to 6
- factor_one: bfloat16 [512, 64], P(('row', 'col')), may hold values from -0.25 to 0.25
- factor_two: bfloat16 [2048, 64], P('col'), may hold values from -0.125 to 0.125
Outputs:
- gram: float32 [256, 256], replicated
All inputs are finite; a program needn't handle non-finite values.
Results may differ from a plain program's by a relative error of at most 0.0003.
Values may be sent and summed in bfloat16 or wider, within the bound.
A program may use at most 64 MiB of HBM per device.

v0:
```python
import jax
import jax.numpy as jnp
from jax import lax
from jax.sharding import PartitionSpec as P

R1 = 64
R2 = 64


def apply_first(partly, first):
    return jnp.einsum(
        "ark,as->srk", partly, first.astype(jnp.float32), precision=lax.Precision.HIGHEST
    )


def per_device(tensor, factor_one, factor_two):
    whole_two = lax.all_gather(factor_two, "col", axis=0, tiled=True)
    partly = jnp.einsum("abk,br->ark", tensor, whole_two, preferred_element_type=jnp.float32)
    scale = R1 * R2
    partial_core = apply_first(partly, factor_one)
    flat_part = partial_core.reshape(R1 * R2, partial_core.shape[2])
    summed = lax.psum(flat_part, ("row", "col"))
    gram = jnp.dot(
        summed.T, summed, precision=lax.Precision.HIGHEST, preferred_element_type=jnp.float32
    )
    return gram / scale


def solution(mesh):
    placed = (P(("row", "col"), None, None), P(("row", "col"), None), P("col", None))
    return jax.shard_map(per_device, mesh=mesh, in_specs=placed, out_specs=P(), check_vma=False)
```

profile of v0, /device:TPU:0, one launch (start us, length us, event | category | flops | bytes accessed | tf_op | source)
XLA Modules:
  0.0 193.5 jit_solution(18068110036583877398)
XLA Ops:
  6.5 0.0 copy-start
  6.5 0.0 all-reduce.2.cloned.1.call-start
  6.5 10.9 %all_gather.3 = bf16[2048,64]{0,1:T(8,128)(2,1)S(1)} all-gather(bf16[512,64]{0,1:T(8,128)(2,1)} %param.5), channel_id=1, replica_groups=mesh['row'=8,'col'=4] {'col'}, dimensions={0}, use_global_device_ids=true | all-gather | bytes 327680 | tf_op jit(solution)/shard_map/all_gather | solution.py:17
  17.4 8.7 %fusion.2 = f32[64,16,256]{2,0,1:T(8,128)S(1)} fusion(bf16[16,2048,256]{2,1,0:T(8,128)(2,1)} %param.3, bf16[2048,64]{0,1:T(8,128)(2,1)S(1)} %all_gather.3), kind=kOutput, calls=%fused_computation.4 | convolution fusion | flops 1073741824 | bytes 18087936 | tf_op jit(solution)/shard_map/abk,br->ark/dot_general | solution.py:18
  26.2 0.0 copy-done
  26.2 2.1 %convolution_bitcast_fusion = f32[64,64,256]{2,0,1:T(8,128)S(1)} fusion(f32[64,16,256]{2,0,1:T(8,128)S(1)} %fusion.2, bf16[16,64]{1,0:T(8,128)(2,1)S(1)} %copy-done), kind=kOutput, calls=%fused_computation | convolution fusion | flops 201326592 | bytes 5244928 | tf_op jit(solution)/shard_map/ark,as->srk/dot_general | solution.py:11
  28.3 4.4 %copy.4 = f32[64,64,256]{2,1,0:T(8,128)} copy(f32[64,64,256]{2,0,1:T(8,128)S(1)} %convolution_bitcast_fusion) | data formatting | bytes 8388608 | tf_op jit(solution)/shard_map/ark,as->srk/dot_general | solution.py:11
  32.7 0.0 all-reduce.2.cloned.1.call-update
  32.7 143.0 %all-reduce.2.cloned.1.call-done = f32[4096,256]{1,0:T(8,128)} async-done(((f32[4096,256]{1,0:T(8,128)}), f32[4096,256]{1,0:T(8,128)}) %all-reduce.2.cloned.1.call-update) | async-done | bytes 4194320 | tf_op jit(solution)/shard_map/psum | solution.py:22
  175.7 10.9 %convolution_multiply_fusion = f32[256,256]{1,0:T(8,128)} fusion(f32[4096,256]{1,0:T(8,128)} %all-reduce.2.cloned.1.call-done), kind=kOutput, calls=%fused_computation.1 | convolution fusion | flops 3221291008 | bytes 4456448 | tf_op jit(solution)/shard_map/dot_general | solution.py:23
Async XLA Ops:
  6.5 19.6 %copy-start = (bf16[16,64]{1,0:T(8,128)(2,1)S(1)}, bf16[16,64]{1,0:T(8,128)(2,1)}, u32[]{:S(2)}) copy-start(bf16[16,64]{1,0:T(8,128)(2,1)} %param.4) | copy-start | bytes 6148
  6.5 169.2 %all-reduce.2.cloned.1.call-start = ((), (), s32[]{:S(2)}) async-start(), calls=%async_computation | async-start | bytes 8388608 | tf_op jit(solution)/shard_map/psum | solution.py:22
Sparse Core Ops, SparseCore 0:
  32.8 142.8 all-reduce.1
where the time goes:
time: 194 us; the launch traced here: 193 us
  waiting for transfers between devices  143 us (74%)
  matrix products  21.8 us (11%)
  between operations  13.4 us (7%)
  blocking collectives  10.9 us (6%)
  local copies, waits for them, and re-layouts  4.39 us (2%)
    psum x1, waiting for transfers between devices, per_device(): summed = lax.psum(flat_part, ('row', 'col'))  143 us
    dot_general x1, matrix products, per_device(): jnp.dot(summed.T, summed, precision=lax.Precision.HIGHEST, preferred_elem...  10.9 us
    all_gather x1, blocking collectives, per_device(): whole_two = lax.all_gather(factor_two, 'col', axis=0, tiled=True)  10.9 us
    dot_general x1, matrix products, per_device(): jnp.einsum('abk,br->ark', tensor, whole_two, preferred_element_type=jnp.f...  8.75 us
    dot_general x1, local copies, waits for them, and re-layouts, apply_first(): jnp.einsum('ark,as->srk', partly, first.astype(jnp.float32), precision=la...  4.39 us
  transfers between devices with their start and end apart: 1, of which 1 were waited for; matrix products, arithmetic and copies ran while one was open for 0% of the time, Pallas kernels for 0%

commit v1 on v0

v1 whole, which is shorter than its diff:
```python
import functools

import jax
import jax.numpy as jnp
from jax import lax
from jax.experimental import pallas as pl
from jax.experimental.pallas import tpu as pltpu
from jax.sharding import PartitionSpec as P

MESH = pl.DeviceIdType.MESH
F32 = jnp.float32
BF16 = jnp.bfloat16
TILE = 8


def over_rows(left, right):
    return lax.dot_general(
        left, right, (((0,), (0,)), ((), ())), preferred_element_type=F32
    )


def split(x):
    high = x.astype(BF16)
    return high, (x - high.astype(F32)).astype(BF16)


def kernel(
    n_col, n, share, copies, owners,
    t_ref, f1_ref, f2_ref, out_ref,
    held, twos, ones, ones_all, stage, recv, part, part_all, total,
    load_sem, two_send, two_recv, one_send, one_recv,
    mid_send, mid_recv, part_send, part_recv, all_send, all_recv,
):
    slab, rank_one = f1_ref.shape
    rank_two = f2_ref.shape[0]
    chunks = stage.shape[1]
    per_chunk = slab // chunks
    my_row, my_col = lax.axis_index("row"), lax.axis_index("col")
    me = my_row * n_col + my_col

    def load(c):
        rows = pl.ds(c * per_chunk, per_chunk)
        return pltpu.make_async_copy(t_ref.at[rows], held.at[rows], load_sem.at[c])

    for c in range(chunks):
        load(c).start()

    barrier = pltpu.get_barrier_semaphore()

    def greet(off, _):
        d = lax.rem(me + off, n)
        pl.semaphore_signal(
            barrier, inc=1, device_id=(d // n_col, lax.rem(d, n_col)), device_id_type=MESH
        )
        return 0

    lax.fori_loop(1, n, greet, 0)

    spread_rows, width = ones.shape
    iota = lambda shape, dim: lax.broadcasted_iota(jnp.int32, shape, dim)
    lanes = iota((rank_one, width), 1)
    repeat = (lax.rem(lanes, rank_one) == iota((rank_one, width), 0)).astype(BF16)
    wide = jnp.dot(f1_ref[...], repeat, preferred_element_type=F32).astype(BF16)
    tall = (iota((spread_rows, slab), 0) // share == iota((spread_rows, slab), 1)).astype(BF16)
    spread = jnp.dot(tall, wide, preferred_element_type=F32)
    keep = iota((spread_rows, width), 1) // rank_one == lax.rem(iota((spread_rows, width), 0), share)
    ones[...] = jnp.where(keep, spread, 0.0).astype(BF16)
    ones_all[me] = ones[...]
    twos[my_col] = f2_ref[...]

    pl.semaphore_wait(barrier, n - 1)

    for off in range(1, n_col):
        pltpu.make_async_remote_copy(
            src_ref=f2_ref, dst_ref=twos.at[my_col],
            send_sem=two_send, recv_sem=two_recv,
            device_id=(my_row, lax.rem(my_col + off, n_col)), device_id_type=MESH,
        ).start()

    def to_all(src, dst, send_sem, recv_sem):
        def one(off, _):
            d = lax.rem(me + off, n)
            pltpu.make_async_remote_copy(
                src_ref=src(d), dst_ref=dst, send_sem=send_sem, recv_sem=recv_sem,
                device_id=(d // n_col, lax.rem(d, n_col)), device_id_type=MESH,
            ).start()
            return 0

        lax.fori_loop(1, n, one, 0)

    def wait_bytes(ref, sem):
        pltpu.make_async_copy(ref, ref, sem).wait()

    to_all(lambda d: ones, ones_all.at[me], one_send, one_recv)
    if n_col > 1:
        wait_bytes(twos.at[pl.ds(0, n_col - 1)], two_recv)
    second = jnp.concatenate([twos[q] for q in range(n_col)], axis=1)

    for c in range(chunks):
        load(c).wait()
        for i in range(per_chunk):
            partly = jnp.dot(second, held[c * per_chunk + i], preferred_element_type=F32)
            for b in range(rank_two // share):
                stage[b, c, pl.ds(i * share, share), :] = partly[b * share:(b + 1) * share, :]
        to_all(lambda d: stage.at[d // copies, c], recv.at[me, c], mid_send, mid_recv)

    recv[me] = stage[me // copies]
    wait_bytes(ones_all.at[pl.ds(0, n - 1)], one_recv)
    wait_bytes(recv.at[pl.ds(0, n - 1)], mid_recv)

    depth = recv.shape[3]
    first = ones_all[...].reshape(n * spread_rows, width)
    high, low = split(recv[...].reshape(n * spread_rows, depth))
    flat = over_rows(first, high) + over_rows(first, low)
    if copies > 1:
        mine = iota(flat.shape, 0) // (rank_one // copies) == lax.rem(me, copies)
        flat = jnp.where(mine, flat, 0.0)
    high, low = split(flat)
    gram = over_rows(high, high) + over_rows(high, low) + over_rows(low, high)
    part[...] = gram.reshape(part.shape)

    def send_part(off, _):
        d = lax.rem(me + off, n)

        @pl.when(d < owners)
        def _():
            pltpu.make_async_remote_copy(
                src_ref=part.at[d], dst_ref=part_all.at[me],
                send_sem=part_send, recv_sem=part_recv,
                device_id=(d // n_col, lax.rem(d, n_col)), device_id_type=MESH,
            ).start()

        return 0

    lax.fori_loop(1, n, send_part, 0)

    @pl.when(me < owners)
    def _():
        part_all[me] = part[me]
        wait_bytes(part_all.at[pl.ds(0, n - 1)], part_recv)
        total[me] = jnp.sum(part_all[...], axis=0)
        to_all(lambda d: total.at[me], total.at[me], all_send, all_recv)
        wait_bytes(total.at[pl.ds(0, owners - 1)], all_recv)
        wait_bytes(part.at[pl.ds(0, owners - 1)], part_send)
        wait_bytes(part_all.at[pl.ds(0, n - 1)], all_send)

    if owners < n:
        @pl.when(me >= owners)
        def _():
            wait_bytes(total, all_recv)
            wait_bytes(part, part_send)

    out_ref[...] = total[...].reshape(out_ref.shape)
    if n_col > 1:
        wait_bytes(twos.at[pl.ds(0, n_col - 1)], two_send)
    wait_bytes(ones_all.at[pl.ds(0, n - 1)], one_send)
    wait_bytes(recv.at[pl.ds(0, n - 1)], mid_send)


def per_device(n_row, n_col, tensor, factor_one, factor_two):
    slab, second_size, depth = tensor.shape
    rank_one, rank_two = factor_one.shape[1], factor_two.shape[1]
    n = n_row * n_col
    share = max(1, rank_two // n)
    copies = max(1, n // rank_two)
    owners = min(n, depth // TILE)
    rows = depth // owners
    chunks = slab * share // TILE
    width = max(128, share * rank_one)
    dma = pltpu.SemaphoreType.DMA
    gram = pl.pallas_call(
        functools.partial(kernel, n_col, n, share, copies, owners),
        out_shape=jax.ShapeDtypeStruct((depth, depth), F32),
        in_specs=[
            pl.BlockSpec(memory_space=pl.ANY),
            pl.BlockSpec(memory_space=pltpu.VMEM),
            pl.BlockSpec(memory_space=pltpu.VMEM),
        ],
        out_specs=pl.BlockSpec(memory_space=pltpu.VMEM),
        scratch_shapes=[
            pltpu.VMEM(tensor.shape, BF16),
            pltpu.VMEM((n_col, rank_two, second_size // n_col), BF16),
            pltpu.VMEM((slab * share, width), BF16),
            pltpu.VMEM((n, slab * share, width), BF16),
            pltpu.VMEM((rank_two // share, chunks, TILE, depth), F32),
            pltpu.VMEM((n, chunks, TILE, depth), F32),
            pltpu.VMEM((owners, rows, depth), F32),
            pltpu.VMEM((n, rows, depth), F32),
            pltpu.VMEM((owners, rows, depth), F32),
            dma((chunks,)),
        ] + [dma] * 10,
        compiler_params=pltpu.CompilerParams(
            collective_id=0, has_side_effects=True, vmem_limit_bytes=60 * 2**20
        ),
        name="project_and_gram",
    )(tensor, factor_one, factor_two.T)
    return gram / (rank_one * rank_two)


def solution(mesh):
    sizes = mesh.shape
    placed = (P(("row", "col"), None, None), P(("row", "col"), None), P("col", None))
    return jax.shard_map(
        functools.partial(per_device, sizes["row"], sizes["col"]),
        mesh=mesh, in_specs=placed, out_specs=P(), check_vma=False,
    )
```

time: 194 us -> 57.4 us (0.30)
  waiting for transfers between devices: 143 us -> 0 us
  Pallas kernels: 0 us -> 55.2 us
  matrix products: 21.8 us -> 0 us
  between operations: 13.4 us -> 0.01 us
  blocking collectives: 10.9 us -> 0 us
  local copies, waits for them, and re-layouts: 4.39 us -> 0 us
    psum x1 -> x0, waiting for transfers between devices: 143 us -> none  [per_device(): summed = lax.psum(flat_part, ('row', 'col'))]
    pallas_call x0 -> x1, Pallas kernels: none -> 55.2 us  [per_device(): pl.pallas_call(functools.partial(kernel, n_col, n, share, copies, owners)...]
    dot_general x3 -> x0, matrix products: 21.8 us -> none  [the longest x1 10.9 us: per_device(): jnp.dot(summed.T, summed, precision=lax.Precision.HIGHEST, preferred_elem...]
    all_gather x1 -> x0, blocking collectives: 10.9 us -> none  [per_device(): whole_two = lax.all_gather(factor_two, 'col', axis=0, tiled=True)]
    dot_general x1 -> x0, local copies, waits for them, and re-layouts: 4.39 us -> none  [apply_first(): jnp.einsum('ark,as->srk', partly, first.astype(jnp.float32), precision=la...]
  transfers between devices with their start and end apart: 1 -> 0, of which waited for: 1 -> 0; matrix products, arithmetic and copies ran while one was open for 0% -> 0% of each run, Pallas kernels for 0% -> 0%
where the time goes in v1:
time: 57.4 us; the launch traced here: 56.9 us
  Pallas kernels  55.2 us (96%)
  other arithmetic  1.67 us (3%)
    pallas_call x1, Pallas kernels, per_device(): pl.pallas_call(functools.partial(kernel, n_col, n, share, copies, owners)...  55.2 us
    div x1, other arithmetic, per_device(): return gram / (rank_one * rank_two)  1.67 us

profile of v1, /device:TPU:0, one launch (start us, length us, event | category | flops | bytes accessed | tf_op | source)
XLA Modules:
  0.0 56.9 jit_solution(12953124983712676560)
XLA Ops:
  0.0 55.2 %project_and_gram.1 = f32[256,256]{1,0:T(8,128)} custom-call(bf16[16,2048,256]{2,1,0:T(8,128)(2,1)} %t_ref.1, bf16[16,64]{1,0:T(8,128)(2,1)} %f1_ref.1, bf16[64,512]{1,0:T(8,128)(2,1)} %bitcast.1), custom_call_target="tpu_custom_call" | custom-call | tf_op jit(solution)/shard_map/project_and_gram/pallas_call | solution.py:171
  55.2 1.7 %broadcast_multiply_fusion = f32[256,256]{1,0:T(8,128)} fusion(f32[256,256]{1,0:T(8,128)} %project_and_gram.1), kind=kLoop, calls=%fused_computation | loop fusion | flops 65536 | bytes 524288 | tf_op jit(solution)/shard_map/div | solution.py:197

commit v2 on v1

v2 whole, which is shorter than its diff:
```python
import functools

import jax
import jax.numpy as jnp
from jax import lax
from jax.experimental import pallas as pl
from jax.experimental.pallas import tpu as pltpu
from jax.sharding import PartitionSpec as P

MESH = pl.DeviceIdType.MESH
F32 = jnp.float32
BF16 = jnp.bfloat16
TILE = 8


def over_rows(left, right):
    return lax.dot_general(
        left, right, (((0,), (0,)), ((), ())), preferred_element_type=F32
    )


def split(x):
    high = x.astype(BF16)
    return high, (x - high.astype(F32)).astype(BF16)


def kernel(
    n_row, n_col, share,
    t_ref, f1_ref, f2_ref, out_ref,
    held, twos, ones, ones_all, spread, stage, recv, outbox, inbox, part, part_all, lines, total,
    load_sem, two_send, two_recv, one_send, one_recv,
    mid_send, mid_recv, box_send, box_recv, part_send, part_recv, line_send, line_recv, all_send, all_recv,
):
    slab, rank_one = f1_ref.shape
    rank_two = f2_ref.shape[0]
    chunks, depth = stage.shape[1], stage.shape[3]
    rows = slab * share
    per_chunk = slab // chunks
    my_row, my_col = lax.axis_index("row"), lax.axis_index("col")
    half_rows = n_row // 2
    n = half_rows * n_col
    my_half, my_seat = my_row // half_rows, lax.rem(my_row, half_rows)
    me = my_seat * n_col + my_col

    def place(d):
        return my_half * half_rows + d // n_col, lax.rem(d, n_col)


    def load(c):
        rows = pl.ds(c * per_chunk, per_chunk)
        return pltpu.make_async_copy(t_ref.at[rows], held.at[rows], load_sem.at[c])

    for c in range(chunks):
        load(c).start()

    barrier = pltpu.get_barrier_semaphore()

    def greet(off, _):
        d = lax.rem(my_row * n_col + my_col + off, 2 * n)
        pl.semaphore_signal(
            barrier, inc=1, device_id=(d // n_col, lax.rem(d, n_col)), device_id_type=MESH
        )
        return 0

    lax.fori_loop(1, 2 * n, greet, 0)

    iota = lambda shape, dim: lax.broadcasted_iota(jnp.int32, shape, dim)
    folds = slab // ones.shape[0]
    ones[...] = jnp.concatenate(
        [f1_ref[pl.ds(q * ones.shape[0], ones.shape[0]), :] for q in range(folds)], axis=1
    )
    ones_all[me] = ones[...]
    twos[my_col] = f2_ref[...]

    pl.semaphore_wait(barrier, 2 * n - 1)

    for off in range(1, n_col):
        pltpu.make_async_remote_copy(
            src_ref=f2_ref, dst_ref=twos.at[my_col],
            send_sem=two_send, recv_sem=two_recv,
            device_id=(my_row, lax.rem(my_col + off, n_col)), device_id_type=MESH,
        ).start()

    def to_all(src, dst, send_sem, recv_sem):
        def one(off, _):
            d = lax.rem(me + off, n)
            pltpu.make_async_remote_copy(
                src_ref=src(d), dst_ref=dst, send_sem=send_sem, recv_sem=recv_sem,
                device_id=place(d), device_id_type=MESH,
            ).start()
            return 0

        lax.fori_loop(1, n, one, 0)

    def wait_bytes(ref, sem):
        pltpu.make_async_copy(ref, ref, sem).wait()

    to_all(lambda d: ones, ones_all.at[me], one_send, one_recv)
    if n_col > 1:
        wait_bytes(twos.at[pl.ds(0, n_col - 1)], two_recv)
    second = jnp.concatenate([twos[q] for q in range(n_col)], axis=1)

    for c in range(chunks):
        load(c).wait()
        for i in range(per_chunk):
            partly = jnp.dot(second, held[c * per_chunk + i], preferred_element_type=F32)
            for b in range(rank_two // share):
                stage[b, c, pl.ds(i * share, share), :] = partly[b * share:(b + 1) * share, :]
        landing = recv.at[pl.ds(pl.multiple_of(me * rows + c * TILE, TILE), TILE)]
        to_all(lambda d: stage.at[d, c], landing, mid_send, mid_recv)

    recv[pl.ds(pl.multiple_of(me * rows, TILE), rows), :] = stage[me].reshape(rows, depth)
    wait_bytes(ones_all.at[pl.ds(0, n - 1)], one_recv)
    packed = ones_all[...].astype(F32)
    whole = jnp.concatenate(
        [packed[:, :, q * rank_one:(q + 1) * rank_one] for q in range(folds)], axis=1
    ).reshape(n * slab, rank_one)
    for j in range(share):
        for w in range(spread.shape[0]):
            parts = [
                whole if w * folds + p == j else jnp.zeros_like(whole) for p in range(folds)
            ]
            spread[w, pl.ds(j, n * slab, stride=share), :] = jnp.concatenate(parts, axis=1)
    first = jnp.concatenate([spread[w] for w in range(spread.shape[0])], axis=1).astype(BF16)
    wait_bytes(recv.at[pl.ds(0, (n - 1) * rows)], mid_recv)

    high, low = split(recv[...])
    flat = over_rows(first, high) + over_rows(first, low)
    outbox[...] = flat[:share * rank_one].reshape(outbox.shape)
    swap = pltpu.make_async_remote_copy(
        src_ref=outbox.at[1 - my_half], dst_ref=inbox, send_sem=box_send, recv_sem=box_recv,
        device_id=(lax.rem(my_row + half_rows, n_row), my_col), device_id_type=MESH,
    )
    swap.start()
    swap.wait_recv()
    flat = outbox[my_half] + inbox[...]
    high, low = split(flat)
    gram = over_rows(high, high) + over_rows(high, low) + over_rows(low, high)
    half = depth // 2
    part[...] = jnp.concatenate(
        [gram[:half, :half], gram[:half, half:], gram[half:, half:]], axis=0
    ).reshape(part.shape)

    plane, planes = part.shape[0], lines.shape[0]
    core, line = lax.rem(my_row, 2), my_row // 2
    seat = core * n_col + my_col

    def mate(off):
        other = lax.rem(seat + off, plane)
        return other, (line * 2 + other // n_col, lax.rem(other, n_col))

    def send(src, dst, send_sem, recv_sem, device):
        pltpu.make_async_remote_copy(
            src_ref=src, dst_ref=dst, send_sem=send_sem, recv_sem=recv_sem,
            device_id=device, device_id_type=MESH,
        ).start()

    for off in range(1, plane):
        other, device = mate(off)
        send(part.at[other], part_all.at[seat], part_send, part_recv, device)
    part_all[seat] = part[seat]
    wait_bytes(part_all.at[pl.ds(0, plane - 1)], part_recv)
    lines[line] = jnp.sum(part_all[...], axis=0)
    for off in range(1, planes):
        device = (lax.rem(line + off, planes) * 2 + core, my_col)
        send(lines.at[line], lines.at[line], line_send, line_recv, device)
    if planes > 1:
        wait_bytes(lines.at[pl.ds(0, planes - 1)], line_recv)
    total[seat] = jnp.sum(lines[...], axis=0)
    for off in range(1, plane):
        _, device = mate(off)
        send(total.at[seat], total.at[seat], all_send, all_recv, device)
    wait_bytes(total.at[pl.ds(0, plane - 1)], all_recv)

    blocks = total[...].reshape(3, half, half)
    out_ref[:half, :half] = blocks[0]
    out_ref[:half, half:] = blocks[1]
    out_ref[half:, :half] = blocks[1].T
    out_ref[half:, half:] = blocks[2]
    swap.wait_send()
    wait_bytes(part_all.at[pl.ds(0, plane - 1)], part_send)
    if planes > 1:
        wait_bytes(lines.at[pl.ds(0, planes - 1)], line_send)
    wait_bytes(total.at[pl.ds(0, plane - 1)], all_send)
    if n_col > 1:
        wait_bytes(twos.at[pl.ds(0, n_col - 1)], two_send)
    wait_bytes(ones_all.at[pl.ds(0, n - 1)], one_send)
    wait_bytes(recv.at[pl.ds(0, (n - 1) * rows)], mid_send)


def per_device(n_row, n_col, tensor, factor_one, factor_two):
    slab, second_size, depth = tensor.shape
    rank_one, rank_two = factor_one.shape[1], factor_two.shape[1]
    n = n_row // 2 * n_col
    share = rank_two // n
    plane, planes = 2 * n_col, n_row // 2
    half = depth // 2
    block = (3 * half // plane, half)
    chunks = slab * share // TILE
    packed = (slab * rank_one // 128, 128)
    dma = pltpu.SemaphoreType.DMA
    gram = pl.pallas_call(
        functools.partial(kernel, n_row, n_col, share),
        out_shape=jax.ShapeDtypeStruct((depth, depth), F32),
        in_specs=[
            pl.BlockSpec(memory_space=pl.ANY),
            pl.BlockSpec(memory_space=pltpu.VMEM),
            pl.BlockSpec(memory_space=pltpu.VMEM),
        ],
        out_specs=pl.BlockSpec(memory_space=pltpu.VMEM),
        scratch_shapes=[
            pltpu.VMEM(tensor.shape, BF16),
            pltpu.VMEM((n_col, rank_two, second_size // n_col), BF16),
            pltpu.VMEM(packed, BF16),
            pltpu.VMEM((n, *packed), BF16),
            pltpu.VMEM((-(-share * rank_one // 128), n * slab * share, 128), F32),
            pltpu.VMEM((rank_two // share, chunks, TILE, depth), F32),
            pltpu.VMEM((n * slab * share, depth), F32),
            pltpu.VMEM((2, share * rank_one // 2, depth), F32),
            pltpu.VMEM((share * rank_one // 2, depth), F32),
            pltpu.VMEM((plane, *block), F32),
            pltpu.VMEM((plane, *block), F32),
            pltpu.VMEM((planes, *block), F32),
            pltpu.VMEM((plane, *block), F32),
            dma((chunks,)),
        ] + [dma] * 14,
        compiler_params=pltpu.CompilerParams(
            collective_id=0, has_side_effects=True, vmem_limit_bytes=60 * 2**20
        ),
        name="project_and_gram",
    )(tensor, factor_one, factor_two.T)
    return gram / (rank_one * rank_two)


def solution(mesh):
    sizes = mesh.shape
    placed = (P(("row", "col"), None, None), P(("row", "col"), None), P("col", None))
    return jax.shard_map(
        functools.partial(per_device, sizes["row"], sizes["col"]),
        mesh=mesh, in_specs=placed, out_specs=P(), check_vma=False,
    )
```

time: 57.4 us -> 50.3 us (0.88)
  Pallas kernels: 55.2 us -> 48.4 us
    pallas_call x1, Pallas kernels: 55.2 us -> 48.4 us  [per_device(): pl.pallas_call(functools.partial(kernel, n_row, n_col, share), out_shape=...]
where the time goes in v2:
time: 50.3 us; the launch traced here: 50.1 us
  Pallas kernels  48.4 us (96%)
  other arithmetic  1.67 us (3%)
    pallas_call x1, Pallas kernels, per_device(): pl.pallas_call(functools.partial(kernel, n_row, n_col, share), out_shape=...  48.4 us
    div x1, other arithmetic, per_device(): return gram / (rank_one * rank_two)  1.67 us

profile of v2, /device:TPU:0, one launch (start us, length us, event | category | flops | bytes accessed | tf_op | source)
XLA Modules:
  0.0 50.1 jit_solution(14926685490004569261)
XLA Ops:
  0.0 48.4 %project_and_gram.1 = f32[256,256]{1,0:T(8,128)} custom-call(bf16[16,2048,256]{2,1,0:T(8,128)(2,1)} %t_ref.1, bf16[16,64]{1,0:T(8,128)(2,1)} %f1_ref.1, bf16[64,512]{1,0:T(8,128)(2,1)} %bitcast.1), custom_call_target="tpu_custom_call" | custom-call | tf_op jit(solution)/shard_map/project_and_gram/pallas_call | solution.py:202
  48.4 1.7 %broadcast_multiply_fusion = f32[256,256]{1,0:T(8,128)} fusion(f32[256,256]{1,0:T(8,128)} %project_and_gram.1), kind=kLoop, calls=%fused_computation | loop fusion | flops 65536 | bytes 524288 | tf_op jit(solution)/shard_map/div | solution.py:232
